TPU v7x, 128 devices: a whole 4x4x4 slice. The times are simulated.
128 devices in a mesh: teacher: 8 (over z_hi, y), student: 16 (over z_lo, x, core).
Axes of the slice: x: 4, y: 4, z: 4 (z_hi: 2, z_lo: 2; z = z_hi * 2 + z_lo), core: 2. Of those that a mesh axis runs over, the one named last changes fastest.
Arguments:
- teacher_in: bfloat16 [16384, 8192], P('student', 'teacher')
- teacher_attn: bfloat16 [16384, 4096], P('student', 'teacher'), may hold values from -6 to 6
- teacher_out_proj: bfloat16 [4096, 8192], P('student', 'teacher'), may hold values from -0.09375 to 0.09375
- teacher_gain: bfloat16 [8192], P('teacher'), may hold values from 0.099609375 to 1.8984375
- projection: bfloat16 [8192, 4096], P('teacher', 'student'), may hold values from -0.0625 to 0.0625
- student_in: bfloat16 [16384, 4096], P('student', 'teacher')
- student_attn: bfloat16 [16384, 2048], P('student', 'teacher'), may hold values from -6 to 6
- student_out_proj: bfloat16 [2048, 4096], P('student', 'teacher'), may hold values from -0.125 to 0.125
- student_gain: bfloat16 [4096], P('teacher'), may hold values from 0.099609375 to 1.8984375
- token_ids: int32 [16384], P('student'), may hold values from 0 to 128004, as said below
- row_order: int32 [16384], replicated, may hold values from 0 to 16383, as said below
Outputs:
- grad_weight: float32 [2048, 4096], P('student', 'teacher')
- grad_gain: float32 [4096], P('teacher')
Inputs may be any that keep to these rules, and one draw needn't show every extreme that they name: `token_ids`: within each sequence of 1024 consecutive rows the rows holding 128004 form the sequence's tail, after at least 256 other rows; no other row holds 128004. `row_order`: A permutation of the 16384 rows. For student block k and teacher block b (blocks of 1024 rows), the entries k * 1024 + b * 64 to k * 1024 + (b + 1) * 64 - 1 name rows of teacher block b.
All inputs are finite; a program needn't handle non-finite values.
Results may differ from a plain program's by a relative error of at most 0.02.
Values may be sent and summed in bfloat16 or wider, within the bound.
A program may use at most 128 MiB of HBM per device.

v0:
```python
import math
import jax
import jax.numpy as jnp
from jax import lax
from jax.sharding import PartitionSpec as P

DT = 8192
DS = 4096
PAD_ID = 128004
epsilon = 1e-05


def rows_first(arrays, axis, dims):
    turned = [jnp.moveaxis(a, dim, 0) for a, dim in zip(arrays, dims)]
    both = jnp.concatenate([t.reshape(len(t), -1) for t in turned], axis=1)
    result, at, outs = (lax.all_gather(both, axis, axis=0, tiled=True), 0, [])
    for t, dim in zip(turned, dims):
        section = result[:, at : at + t[0].size].reshape(-1, *t.shape[1:])
        outs.append(jnp.moveaxis(section, 0, dim))
        at += t[0].size
    return tuple(outs)


def sent_to_all(array, axis):
    peers = lax.axis_size(axis)
    return lax.all_to_all(
        jnp.broadcast_to(array[None], (peers, *array.shape)), axis, 0, 0, tiled=True
    )


def of_everyone(array, axis):
    everything = sent_to_all(array, axis)
    return jnp.sum(everything, axis=0)


def sent_together(arrays, axis, split_dim, concat_dim, along):
    columns = [a.reshape(*a.shape[:along], -1) for a in arrays]
    both = jnp.concatenate(columns, axis=along)
    result, at, outs = (
        lax.all_to_all(both, axis, split_axis=split_dim, concat_axis=concat_dim, tiled=True),
        0,
        [],
    )
    for a, column in zip(arrays, columns):
        section = result[..., at : at + column.shape[along]]
        outs.append(section.reshape(*section.shape[:along], *a.shape[along:]))
        at += column.shape[along]
    return tuple(outs)


def in_blocks(array, dim, peers):
    shape = array.shape
    parts = array.reshape(*shape[:dim], peers, shape[dim] // peers, *shape[dim + 1 :])
    return jnp.moveaxis(parts, dim, 0)


def sent_and_summed(array, axis, dim):
    peers = lax.axis_size(axis)
    parts = lax.all_to_all(in_blocks(array, dim, peers), axis, 0, 0, tiled=True)
    return jnp.sum(parts.astype(jnp.float32), axis=0)


def shards(
    teacher_in,
    teacher_attn,
    teacher_out_proj,
    teacher_gain,
    projection,
    student_in,
    student_attn,
    student_out_proj,
    student_gain,
    token_ids,
    row_order,
):
    student_count = lax.axis_size("student")
    teacher_count = lax.axis_size("teacher")
    row_count = teacher_in.shape[0]
    piece_rows = row_count // student_count
    student_index = lax.axis_index("student")
    attn_all = lax.all_gather(teacher_attn, "teacher", axis=1, tiled=True)
    out_full, proj_full = rows_first((teacher_out_proj, projection), "student", (0, 1))
    branch = jnp.dot(attn_all, out_full, preferred_element_type=jnp.float32)
    residual = teacher_in.astype(jnp.float32) + branch
    square_sum = of_everyone(jnp.sum(residual * residual, axis=1), "teacher")
    teacher_scale = lax.rsqrt(square_sum / DT + epsilon)
    hidden = (residual * teacher_scale[:, None] * teacher_gain.astype(jnp.float32)[None, :]).astype(
        jnp.bfloat16
    )
    proj_blocks = proj_full.reshape(
        proj_full.shape[0], teacher_count, proj_full.shape[1] // teacher_count
    )
    row_blocks = row_order.reshape(student_count, student_count, piece_rows)
    local_rows = (
        lax.dynamic_index_in_dim(row_blocks, student_index, 1, keepdims=False)
        - student_index * row_count
    )
    live_rows = jnp.where(token_ids != PAD_ID, 1.0, 0.0).astype(jnp.bfloat16)
    mask_send = jnp.take(live_rows, local_rows, axis=0)
    columns = proj_blocks
    summed = lax.psum_scatter(
        jnp.einsum("tf,fko->kto", hidden, columns, preferred_element_type=jnp.float32).astype(
            jnp.bfloat16
        ),
        "teacher",
        scatter_dimension=0,
        tiled=True,
    ).astype(jnp.float32)
    target_rows = summed[0].astype(jnp.bfloat16)
    moved, mask_got = sent_together(
        (jnp.take(target_rows, local_rows, axis=0), mask_send), "student", 0, 0, 2
    )
    target = moved.reshape(row_count, moved.shape[2])
    weight_mask = mask_got.reshape(row_count).astype(jnp.float32)
    attn_student = lax.all_gather(student_attn, "teacher", axis=1, tiled=True)
    columns = attn_student
    student_branch = jnp.dot(
        columns,
        lax.all_gather(student_out_proj, "student", axis=0, tiled=True),
        preferred_element_type=jnp.float32,
    )
    student_res = student_in.astype(jnp.float32) + student_branch
    student_square = of_everyone(jnp.sum(student_res * student_res, axis=1), "teacher")
    student_scale = lax.rsqrt(student_square / DS + epsilon)
    normed = student_res * student_scale[:, None]
    gain_values = student_gain.astype(jnp.float32)[None, :]
    distance = normed * gain_values - target.astype(jnp.float32)
    loss_weight = 1.0 / math.sqrt(row_count * student_count)
    grad_out = distance * (weight_mask * loss_weight)[:, None]
    gain_part = jnp.sum(grad_out * normed, axis=0)
    grad_norm = grad_out * gain_values
    inner_sum = of_everyone(jnp.sum(grad_norm * normed, axis=1), "teacher")
    grad_res = (student_scale[:, None] * (grad_norm - normed * (inner_sum / DS)[:, None])).astype(
        jnp.bfloat16
    )
    columns = attn_student
    grad_weight = sent_and_summed(
        lax.dot_general(
            columns, grad_res, (((0,), (0,)), ((), ())), preferred_element_type=jnp.float32
        ).astype(jnp.bfloat16),
        "student",
        0,
    )
    grad_gain = of_everyone(gain_part, "student")
    return (grad_weight, grad_gain)


def solution(mesh):
    placed = (
        P("student", "teacher"),
        P("student", "teacher"),
        P("student", "teacher"),
        P("teacher"),
        P("teacher", "student"),
        P("student", "teacher"),
        P("student", "teacher"),
        P("student", "teacher"),
        P("teacher"),
        P("student"),
        P(),
    )
    return jax.shard_map(
        shards,
        mesh=mesh,
        in_specs=placed,
        out_specs=(P("student", "teacher"), P("teacher")),
        check_vma=False,
    )
```

profile of v0, /device:TPU:3, one launch (start us, length us, event | category | flops | bytes accessed | tf_op | source)
XLA Modules:
  0.0 564.8 jit_solution(5684495137640013331)
XLA Ops:
  7.2 0.7 all-gather.11.cloned.1.call-update
  8.0 1.2 copy.60
  9.2 1.1 pad_maximum_fusion.1
  11.7 2.6 copy.62
  14.3 116.5 %all-gather.11.cloned.1.call-done = bf16[1024,4096]{1,0:T(8,128)(2,1)} async-done(((bf16[1024,512]{1,0:T(8,128)(2,1)}), bf16[1024,4096]{1,0:T(8,128)(2,1)}) %all-gather.11.cloned.1.call-update) | async-done | bytes 8388624 | tf_op jit(solution)/shard_map/all_gather | solution.py:81
  130.8 99.5 %all-gather.9.cloned.1.call-done = bf16[4096,2048]{0,1:T(8,128)(2,1)} async-done(((bf16[256,2048]{0,1:T(8,128)(2,1)}), bf16[4096,2048]{0,1:T(8,128)(2,1)}) %all-gather.9.cloned.1.call-update) | async-done | bytes 16777232 | tf_op jit(solution)/shard_map/all_gather | solution.py:16
  230.3 15.4 %multiply_reduce_fusion = (f32[1024]{0:T(1024)S(1)}, f32[1024,1024]{1,0:T(8,128)}) fusion(bf16[1024,1024]{0,1:T(8,128)(2,1)} %copy.62, bf16[1024,4096]{1,0:T(8,128)(2,1)} %all-gather.11.cloned.1.call-done, bf16[4096,2048]{0,1:T(8,128)(2,1)} %all-gather.9.cloned.1.call-done), kind=kOutput, calls=%fused_computation.9 | convolution fusion | flops 8594127872 | bytes 23072768 | tf_op jit(solution)/shard_map/dot_general | solution.py:83
  246.4 6.3 %all-to-all-start.1 = ((f32[8,1,1024]{2,1,0:T(1,128)}), f32[8,1,1024]{2,1,0:T(1,128)S(1)}, u32[]{:S(2)}, u32[]{:S(2)}) async-start(f32[8,1,1024]{2,1,0:T(1,128)} %broadcast_in_dim.34), calls=%async_computation.1 | async-start | bytes 65536 | tf_op jit(solution)/shard_map/all_to_all | solution.py:26
  252.9 7.8 %slice_bitcast_fusion = bf16[1024,4096]{1,0:T(8,128)(2,1)} fusion(bf16[4096,2048]{0,1:T(8,128)(2,1)} %all-gather.9.cloned.1.call-done), kind=kLoop, calls=%fused_computation.4 | loop fusion | bytes 16777216 | tf_op jit(solution)/shard_map/transpose | solution.py:19
  260.7 12.1 %copy.61 = bf16[1024,4096]{0,1:T(8,128)(2,1)} copy(bf16[1024,4096]{1,0:T(8,128)(2,1)} %slice_bitcast_fusion) | data formatting | bytes 16777216 | tf_op jit(solution)/shard_map/transpose | solution.py:19
  272.9 15.4 %convert_bitcast_fusion = bf16[8,1024,512]{1,2,0:T(8,128)(2,1)} fusion(bf16[1024,8,512]{0,2,1:T(8,128)(2,1)} %bitcast.38, f32[1024,1024]{1,0:T(8,128)} %get-tuple-element.11, bf16[1024,1024]{0,1:T(8,128)(2,1)S(1)} %copy-done.1, f32[1024]{0:T(1024)S(1)} %convert_element_type.58, f32[1024]{0:T(1024)S(1)} %add_rsqrt_fusion), kind=kOutput, calls=%fused_computation.5 | convolution fusion | flops 8599371776 | bytes 23076864 | tf_op jit(solution)/shard_map/tf,fko->kto/dot_general | solution.py:102
  288.4 0.8 copy-done.4
  289.4 6.8 %gather_fusion.1 = bf16[1024]{0:T(1024)(128)(2,1)S(1)} fusion(bf16[1024]{0:T(1024)(128)(2,1)S(1)} %select_convert_fusion, s32[1024]{0:T(1024)S(1)} %broadcast_clamp_fusion), kind=kCustom, calls=%fused_computation.1 | custom fusion | bytes 8192 | tf_op jit(solution)/shard_map/jit(_take)/gather | solution.py:99
  297.1 46.7 %all-gather.5.cloned.1.call-done = bf16[1024,2048]{1,0:T(8,128)(2,1)} async-done(((bf16[1024,256]{1,0:T(8,128)(2,1)}), bf16[1024,2048]{1,0:T(8,128)(2,1)}) %all-gather.5.cloned.1.call-update) | async-done | bytes 4194320 | tf_op jit(solution)/shard_map/all_gather | solution.py:115
  343.9 6.6 %multiply_reduce_fusion.3 = (f32[1024]{0:T(1024)S(1)}, f32[1024,512]{0,1:T(8,128)}) fusion(bf16[1024,2048]{1,0:T(8,128)(2,1)} %all-gather.5.cloned.1.call-done, bf16[2048,512]{1,0:T(8,128)(2,1)} %all-gather.7.cloned.1.call-done, bf16[1024,512]{0,1:T(8,128)(2,1)S(1)} %copy.58), kind=kOutput, calls=%fused_computation.19 | convolution fusion | flops 2149579776 | bytes 9441280 | tf_op jit(solution)/shard_map/dot_general | solution.py:117
  351.1 3.4 all-to-all-start
  354.5 107.1 %reduce-scatter.2.cloned.1.call-done = bf16[1,1024,512]{1,2,0:T(8,128)(2,1)} async-done(((bf16[8,1024,512]{1,2,0:T(8,128)(2,1)}), bf16[1,1024,512]{1,2,0:T(8,128)(2,1)}) %reduce-scatter.2.cloned.1.call-update) | async-done | bytes 1048592 | tf_op jit(solution)/shard_map/reduce_scatter | solution.py:101
  461.6 1.5 copy.65
  463.1 4.0 gather_fusion
  467.3 1.2 pad_maximum_fusion
  468.4 5.9 %all-to-all-start.2 = ((bf16[16,64,513]{2,1,0:T(8,128)(2,1)}), bf16[16,64,513]{2,1,0:T(8,128)(2,1)S(1)}, u32[]{:S(2)}, u32[]{:S(2)}) async-start(bf16[16,64,513]{2,1,0:T(8,128)(2,1)} %pad_maximum_fusion), calls=%async_computation.3 | async-start | bytes 2621440 | tf_op jit(solution)/shard_map/all_to_all | solution.py:40
  474.5 16.8 %all-to-all-done.2 = bf16[16,64,513]{2,1,0:T(8,128)(2,1)S(1)} async-done(((bf16[16,64,513]{2,1,0:T(8,128)(2,1)}), bf16[16,64,513]{2,1,0:T(8,128)(2,1)S(1)}, u32[]{:S(2)}, u32[]{:S(2)}) %all-to-all-start.2) | async-done | bytes 1050656 | tf_op jit(solution)/shard_map/all_to_all | solution.py:40
  491.3 1.7 bitcast_convert_fusion
  493.0 1.9 copy.67
  495.2 2.4 multiply_reduce_fusion.1
  497.6 10.2 %all_to_all.34 = f32[8,1,1024]{2,1,0:T(1,128)S(1)} all-to-all(f32[8,1,1024]{2,1,0:T(1,128)S(1)} %broadcast_in_dim.62), channel_id=1, replica_groups=mesh['teacher'=8,'student'=16] {'teacher'}, dimensions={0} | all-to-all | bytes 65536 | tf_op jit(solution)/shard_map/all_to_all | solution.py:26
  508.4 7.2 %all-to-all-start.5 = ((f32[16,1,512]{2,1,0:T(1,128)}), f32[16,1,512]{2,1,0:T(1,128)S(1)}, u32[]{:S(2)}, u32[]{:S(2)}) async-start(f32[16,1,512]{2,1,0:T(1,128)} %broadcast_in_dim.63), calls=%async_computation.6 | async-start | bytes 65536 | tf_op jit(solution)/shard_map/all_to_all | solution.py:26
  515.7 5.4 fusion.6
  521.1 1.9 copy.82
  523.0 5.8 %all-to-all-start.4 = ((bf16[16,128,512]{1,2,0:T(8,128)(2,1)}), bf16[16,128,512]{1,2,0:T(8,128)(2,1)S(1)}, u32[]{:S(2)}, u32[]{:S(2)}) async-start(bf16[16,128,512]{1,2,0:T(8,128)(2,1)} %bitcast.37), calls=%async_computation.5 | async-start | bytes 4194304 | tf_op jit(solution)/shard_map/all_to_all | solution.py:59
  529.4 27.7 %all-to-all-done.4 = bf16[16,128,512]{1,2,0:T(8,128)(2,1)S(1)} async-done(((bf16[16,128,512]{1,2,0:T(8,128)(2,1)}), bf16[16,128,512]{1,2,0:T(8,128)(2,1)S(1)}, u32[]{:S(2)}, u32[]{:S(2)}) %all-to-all-start.4) | async-done | bytes 2097184 | tf_op jit(solution)/shard_map/all_to_all | solution.py:59
  557.4 0.8 copy.72
  (57 shorter events, 6.2 us)
Async XLA Ops:
  7.2 2.1 copy-start.3
  7.2 123.6 %all-gather.11.cloned.1.call-start = ((), (), s32[]{:S(2)}) async-start(), calls=%async_computation.10 | async-start | bytes 9437184 | tf_op jit(solution)/shard_map/all_gather | solution.py:81
  7.9 222.4 %all-gather.9.cloned.1.call-start = ((), (), s32[]{:S(2)}) async-start(), calls=%async_computation.9 | async-start | bytes 17825792 | tf_op jit(solution)/shard_map/all_gather | solution.py:16
  9.2 2.5 copy-start
  10.4 286.8 %all-gather.7.cloned.1.call-start = ((), (), s32[]{:S(2)}) async-start(), calls=%async_computation.8 | async-start | bytes 2228224 | tf_op jit(solution)/shard_map/all_gather | solution.py:119
  11.1 332.8 %all-gather.5.cloned.1.call-start = ((), (), s32[]{:S(2)}) async-start(), calls=%async_computation.7 | async-start | bytes 4718592 | tf_op jit(solution)/shard_map/all_gather | solution.py:115
  11.7 2.6 copy-start.6
  246.4 26.5 %all-to-all-start.1 = ((f32[8,1,1024]{2,1,0:T(1,128)}), f32[8,1,1024]{2,1,0:T(1,128)S(1)}, u32[]{:S(2)}, u32[]{:S(2)}) async-start(f32[8,1,1024]{2,1,0:T(1,128)} %broadcast_in_dim.34), calls=%async_computation.1 | async-start | bytes 65536 | tf_op jit(solution)/shard_map/all_to_all | solution.py:26
  252.7 208.9 %reduce-scatter.2.cloned.1.call-start = ((), (), s32[]{:S(2)}) async-start(), calls=%async_computation.11 | async-start | bytes 9437184 | tf_op jit(solution)/shard_map/reduce_scatter | solution.py:101
  260.7 12.2 %copy-start.1 = (bf16[1024,1024]{0,1:T(8,128)(2,1)S(1)}, bf16[1024,1024]{0,1:T(8,128)(2,1)}, u32[]{:S(2)}) copy-start(bf16[1024,1024]{0,1:T(8,128)(2,1)} %copy.62) | copy-start | bytes 6291460
  288.4 0.8 copy-start.4
  288.4 1.0 copy-start.5
  289.4 7.1 %copy-start.2 = (bf16[1024,512]{1,0:T(8,128)(2,1)S(1)}, bf16[1024,512]{1,0:T(8,128)(2,1)}, u32[]{:S(2)}) copy-start(bf16[1024,512]{1,0:T(8,128)(2,1)} %param.16) | copy-start | bytes 3145732
  351.1 117.4 %all-to-all-start = ((f32[8,1,1024]{2,1,0:T(1,128)}), f32[8,1,1024]{2,1,0:T(1,128)S(1)}, u32[]{:S(2)}, u32[]{:S(2)}) async-start(f32[8,1,1024]{2,1,0:T(1,128)} %broadcast_in_dim.32), calls=%async_computation | async-start | bytes 65536 | tf_op jit(solution)/shard_map/all_to_all | solution.py:26
  467.2 7.2 %copy-start.7 = (bf16[512]{0:T(512)(128)(2,1)S(1)}, bf16[512]{0:T(512)(128)(2,1)}, u32[]{:S(2)}) copy-start(bf16[512]{0:T(512)(128)(2,1)} %param.19) | copy-start | bytes 3076
  468.4 22.8 %all-to-all-start.2 = ((bf16[16,64,513]{2,1,0:T(8,128)(2,1)}), bf16[16,64,513]{2,1,0:T(8,128)(2,1)S(1)}, u32[]{:S(2)}, u32[]{:S(2)}) async-start(bf16[16,64,513]{2,1,0:T(8,128)(2,1)} %pad_maximum_fusion), calls=%async_computation.3 | async-start | bytes 2621440 | tf_op jit(solution)/shard_map/all_to_all | solution.py:40
  508.4 14.5 %all-to-all-start.5 = ((f32[16,1,512]{2,1,0:T(1,128)}), f32[16,1,512]{2,1,0:T(1,128)S(1)}, u32[]{:S(2)}, u32[]{:S(2)}) async-start(f32[16,1,512]{2,1,0:T(1,128)} %broadcast_in_dim.63), calls=%async_computation.6 | async-start | bytes 65536 | tf_op jit(solution)/shard_map/all_to_all | solution.py:26
  523.0 34.1 %all-to-all-start.4 = ((bf16[16,128,512]{1,2,0:T(8,128)(2,1)}), bf16[16,128,512]{1,2,0:T(8,128)(2,1)S(1)}, u32[]{:S(2)}, u32[]{:S(2)}) async-start(bf16[16,128,512]{1,2,0:T(8,128)(2,1)} %bitcast.37), calls=%async_computation.5 | async-start | bytes 4194304 | tf_op jit(solution)/shard_map/all_to_all | solution.py:59
Sparse Core Ops, SparseCore 0:
  10.2 120.5 all-gather.10
  132.4 97.8 all-gather.8
  232.0 33.8 all-gather.6
  267.9 75.8 all-gather.4
  347.6 113.9 reduce-scatter.1
where the time goes:
time: 566 us; the launch traced here: 565 us
  waiting for transfers between devices  416 us (73%)
  local copies, waits for them, and re-layouts  44.6 us (8%)
  matrix products  42.8 us (8%)
  starting transfers between devices  29.1 us (5%)
  between operations  14 us (2%)
  blocking collectives  10.2 us (2%)
  other arithmetic  7.84 us (1%)
    all_gather x1, waiting for transfers between devices, shards(): attn_all = lax.all_gather(teacher_attn, 'teacher', axis=1, tiled=True)  117 us
    reduce_scatter x1, waiting for transfers between devices, shards(): lax.psum_scatter(jnp.einsum('tf,fko->kto', hidden, columns, preferred_ele...  107 us
    all_gather x1, waiting for transfers between devices, rows_first(): result, at, outs = (lax.all_gather(both, axis, axis=0, tiled=True), 0, [])  99.5 us
    all_gather x1, waiting for transfers between devices, shards(): attn_student = lax.all_gather(student_attn, 'teacher', axis=1, tiled=True)  46.7 us
    all_to_all x1, waiting for transfers between devices, sent_and_summed(): parts = lax.all_to_all(in_blocks(array, dim, peers), axis, 0, 0, tiled=True)  27.7 us
    transpose x2, local copies, waits for them, and re-layouts, rows_first(): outs.append(jnp.moveaxis(section, 0, dim))  20 us
    all_to_all x3, starting transfers between devices, sent_to_all(): lax.all_to_all(jnp.broadcast_to(array[None], (peers, *array.shape)), axis...  17 us
    all_to_all x1, waiting for transfers between devices, sent_together(): lax.all_to_all(both, axis, split_axis=split_dim, concat_axis=concat_dim,...  16.8 us
  transfers between devices with their start and end apart: 10, of which 6 were waited for; matrix products, arithmetic and copies ran while one was open for 15% of the time, Pallas kernels for 0%

commit v1 on v0

--- a/solution.py
+++ b/solution.py
@@ -112,7 +112,10 @@
     )
     target = moved.reshape(row_count, moved.shape[2])
     weight_mask = mask_got.reshape(row_count).astype(jnp.float32)
-    attn_student = lax.all_gather(student_attn, "teacher", axis=1, tiled=True)
+    attn_student = jnp.concatenate(
+        lax.all_to_all(jnp.stack([student_attn] * lax.axis_size("teacher")), "teacher", 0, 0),
+        axis=1,
+    )
     columns = attn_student
     student_branch = jnp.dot(
         columns,

time: 566 us -> 560 us (0.989)
  waiting for transfers between devices: 416 us -> 391 us
  starting transfers between devices: 29.1 us -> 45.6 us
    all_to_all x0 -> x1, waiting for transfers between devices: none -> 57.9 us  [shards(): lax.all_to_all(jnp.stack([student_attn] * lax.axis_size('teacher')), 'tea...]
    all_gather x1 -> x0, waiting for transfers between devices: 46.7 us -> none  [shards(): attn_student = lax.all_gather(student_attn, 'teacher', axis=1, tiled=True)]
    reduce_scatter x1, waiting for transfers between devices: 107 us -> 71.1 us  [shards(): lax.psum_scatter(jnp.einsum('tf,fko->kto', hidden, columns, preferred_ele...]
    all_to_all x3, starting transfers between devices: 17 us -> 27 us  [sent_to_all(): lax.all_to_all(jnp.broadcast_to(array[None], (peers, *array.shape)), axis...]
    all_to_all x0 -> x1, starting transfers between devices: none -> 6.74 us  [shards(): lax.all_to_all(jnp.stack([student_attn] * lax.axis_size('teacher')), 'tea...]
  transfers between devices with their start and end apart: 10 -> 10, of which waited for: 6 -> 6; matrix products, arithmetic and copies ran while one was open for 15% -> 16% of each run, Pallas kernels for 0% -> 0%
where the time goes in v1:
time: 560 us; the launch traced here: 559 us
  waiting for transfers between devices  391 us (70%)
  local copies, waits for them, and re-layouts  47.6 us (8%)
  starting transfers between devices  45.6 us (8%)
  matrix products  42.7 us (8%)
  between operations  14 us (2%)
  blocking collectives  10.2 us (2%)
  other arithmetic  7.85 us (1%)
    all_gather x1, waiting for transfers between devices, shards(): attn_all = lax.all_gather(teacher_attn, 'teacher', axis=1, tiled=True)  117 us
    all_gather x1, waiting for transfers between devices, rows_first(): result, at, outs = (lax.all_gather(both, axis, axis=0, tiled=True), 0, [])  99.5 us
    reduce_scatter x1, waiting for transfers between devices, shards(): lax.psum_scatter(jnp.einsum('tf,fko->kto', hidden, columns, preferred_ele...  71.1 us
    all_to_all x1, waiting for transfers between devices, shards(): lax.all_to_all(jnp.stack([student_attn] * lax.axis_size('teacher')), 'tea...  57.9 us
    all_to_all x1, waiting for transfers between devices, sent_and_summed(): parts = lax.all_to_all(in_blocks(array, dim, peers), axis, 0, 0, tiled=True)  27.7 us
    all_to_all x3, starting transfers between devices, sent_to_all(): lax.all_to_all(jnp.broadcast_to(array[None], (peers, *array.shape)), axis...  27 us
    transpose x2, local copies, waits for them, and re-layouts, rows_first(): outs.append(jnp.moveaxis(section, 0, dim))  19.9 us
    all_to_all x1, waiting for transfers between devices, sent_together(): lax.all_to_all(both, axis, split_axis=split_dim, concat_axis=concat_dim,...  16.8 us
  transfers between devices with their start and end apart: 10, of which 6 were waited for; matrix products, arithmetic and copies ran while one was open for 16% of the time, Pallas kernels for 0%

profile of v1, /device:TPU:3, one launch (start us, length us, event | category | flops | bytes accessed | tf_op | source)
XLA Modules:
  0.0 559.3 jit_solution(820895618791627433)
XLA Ops:
  8.0 1.4 copy.65
  9.4 1.1 pad_maximum_fusion.1
  11.3 2.6 copy.67
  13.8 117.0 %all-gather.8.cloned.1.call-done = bf16[1024,4096]{1,0:T(8,128)(2,1)} async-done(((bf16[1024,512]{1,0:T(8,128)(2,1)}), bf16[1024,4096]{1,0:T(8,128)(2,1)}) %all-gather.8.cloned.1.call-update) | async-done | bytes 8388624 | tf_op jit(solution)/shard_map/all_gather | solution.py:81
  130.8 99.5 %all-gather.6.cloned.1.call-done = bf16[4096,2048]{0,1:T(8,128)(2,1)} async-done(((bf16[256,2048]{0,1:T(8,128)(2,1)}), bf16[4096,2048]{0,1:T(8,128)(2,1)}) %all-gather.6.cloned.1.call-update) | async-done | bytes 16777232 | tf_op jit(solution)/shard_map/all_gather | solution.py:16
  230.3 15.4 %multiply_reduce_fusion = (f32[1024]{0:T(1024)S(1)}, f32[1024,1024]{1,0:T(8,128)}) fusion(bf16[1024,1024]{0,1:T(8,128)(2,1)} %copy.67, bf16[1024,4096]{1,0:T(8,128)(2,1)} %all-gather.8.cloned.1.call-done, bf16[4096,2048]{0,1:T(8,128)(2,1)} %all-gather.6.cloned.1.call-done), kind=kOutput, calls=%fused_computation.9 | convolution fusion | flops 8594127872 | bytes 23072768 | tf_op jit(solution)/shard_map/dot_general | solution.py:83
  246.4 6.3 %all-to-all-start.2 = ((f32[8,1,1024]{2,1,0:T(1,128)}), f32[8,1,1024]{2,1,0:T(1,128)S(1)}, u32[]{:S(2)}, u32[]{:S(2)}) async-start(f32[8,1,1024]{2,1,0:T(1,128)} %broadcast_in_dim.34), calls=%async_computation.2 | async-start | bytes 65536 | tf_op jit(solution)/shard_map/all_to_all | solution.py:26
  252.7 7.8 %slice_bitcast_fusion = bf16[1024,4096]{1,0:T(8,128)(2,1)} fusion(bf16[4096,2048]{0,1:T(8,128)(2,1)} %all-gather.6.cloned.1.call-done), kind=kLoop, calls=%fused_computation.4 | loop fusion | bytes 16777216 | tf_op jit(solution)/shard_map/transpose | solution.py:19
  260.5 12.1 %copy.66 = bf16[1024,4096]{0,1:T(8,128)(2,1)} copy(bf16[1024,4096]{1,0:T(8,128)(2,1)} %slice_bitcast_fusion) | data formatting | bytes 16777216 | tf_op jit(solution)/shard_map/transpose | solution.py:19
  272.7 15.4 %convert_bitcast_fusion = bf16[8,1024,512]{1,2,0:T(8,128)(2,1)} fusion(bf16[1024,8,512]{0,2,1:T(8,128)(2,1)} %bitcast.41, f32[1024,1024]{1,0:T(8,128)} %get-tuple-element.11, bf16[1024,1024]{0,1:T(8,128)(2,1)S(1)} %copy-done.1, f32[1024]{0:T(1024)S(1)} %convert_element_type.58, f32[1024]{0:T(1024)S(1)} %add_rsqrt_fusion), kind=kOutput, calls=%fused_computation.5 | convolution fusion | flops 8599371776 | bytes 23076864 | tf_op jit(solution)/shard_map/tf,fko->kto/dot_general | solution.py:102
  288.1 1.0 copy-done.3
  289.4 2.5 stack.2
  291.8 6.7 %all-to-all-start = ((bf16[8,1024,256]{1,2,0:T(8,128)(2,1)}), bf16[8,1024,256]{1,2,0:T(8,128)(2,1)}, u32[]{:S(2)}, u32[]{:S(2)}) async-start(bf16[8,1024,256]{1,2,0:T(8,128)(2,1)} %stack.2), calls=%async_computation | async-start | bytes 8388608 | tf_op jit(solution)/shard_map/all_to_all | solution.py:116
  298.8 6.8 %gather_fusion.1 = bf16[1024]{0:T(1024)(128)(2,1)S(1)} fusion(bf16[1024]{0:T(1024)(128)(2,1)S(1)} %select_convert_fusion, s32[1024]{0:T(1024)S(1)} %broadcast_clamp_fusion), kind=kCustom, calls=%fused_computation.1 | custom fusion | bytes 8192 | tf_op jit(solution)/shard_map/jit(_take)/gather | solution.py:99
  306.5 57.9 %all-to-all-done = bf16[8,1024,256]{1,2,0:T(8,128)(2,1)} async-done(((bf16[8,1024,256]{1,2,0:T(8,128)(2,1)}), bf16[8,1024,256]{1,2,0:T(8,128)(2,1)}, u32[]{:S(2)}, u32[]{:S(2)}) %all-to-all-start) | async-done | bytes 4194336 | tf_op jit(solution)/shard_map/all_to_all | solution.py:116
  364.4 6.6 %multiply_reduce_fusion.3 = (f32[1024]{0:T(1024)S(1)}, f32[1024,512]{0,1:T(8,128)}) fusion(bf16[1024,2048]{0,1:T(8,128)(2,1)} %bitcast.1, bf16[2048,512]{1,0:T(8,128)(2,1)} %all-gather.4.cloned.1.call-done, bf16[1024,512]{0,1:T(8,128)(2,1)S(1)} %copy.62), kind=kOutput, calls=%fused_computation.19 | convolution fusion | flops 2149579776 | bytes 9441280 | tf_op jit(solution)/shard_map/dot_general | solution.py:120
  371.6 13.5 %all-to-all-start.1 = ((f32[8,1,1024]{2,1,0:T(1,128)}), f32[8,1,1024]{2,1,0:T(1,128)S(1)}, u32[]{:S(2)}, u32[]{:S(2)}) async-start(f32[8,1,1024]{2,1,0:T(1,128)} %broadcast_in_dim.32), calls=%async_computation.1 | async-start | bytes 65536 | tf_op jit(solution)/shard_map/all_to_all | solution.py:26
  385.1 71.1 %reduce-scatter.2.cloned.1.call-done = bf16[1,1024,512]{1,2,0:T(8,128)(2,1)} async-done(((bf16[8,1024,512]{1,2,0:T(8,128)(2,1)}), bf16[1,1024,512]{1,2,0:T(8,128)(2,1)}) %reduce-scatter.2.cloned.1.call-update) | async-done | bytes 1048592 | tf_op jit(solution)/shard_map/reduce_scatter | solution.py:101
  456.1 1.5 copy.70
  457.6 4.0 gather_fusion
  461.8 1.2 pad_maximum_fusion
  463.0 5.9 %all-to-all-start.3 = ((bf16[16,64,513]{2,1,0:T(8,128)(2,1)}), bf16[16,64,513]{2,1,0:T(8,128)(2,1)S(1)}, u32[]{:S(2)}, u32[]{:S(2)}) async-start(bf16[16,64,513]{2,1,0:T(8,128)(2,1)} %pad_maximum_fusion), calls=%async_computation.4 | async-start | bytes 2621440 | tf_op jit(solution)/shard_map/all_to_all | solution.py:40
  469.0 16.8 %all-to-all-done.3 = bf16[16,64,513]{2,1,0:T(8,128)(2,1)S(1)} async-done(((bf16[16,64,513]{2,1,0:T(8,128)(2,1)}), bf16[16,64,513]{2,1,0:T(8,128)(2,1)S(1)}, u32[]{:S(2)}, u32[]{:S(2)}) %all-to-all-start.3) | async-done | bytes 1050656 | tf_op jit(solution)/shard_map/all_to_all | solution.py:40
  485.9 1.7 bitcast_convert_fusion
  487.6 1.9 copy.72
  489.8 2.4 multiply_reduce_fusion.1
  492.2 10.2 %all_to_all.39 = f32[8,1,1024]{2,1,0:T(1,128)S(1)} all-to-all(f32[8,1,1024]{2,1,0:T(1,128)S(1)} %broadcast_in_dim.62), channel_id=1, replica_groups=mesh['teacher'=8,'student'=16] {'teacher'}, dimensions={0} | all-to-all | bytes 65536 | tf_op jit(solution)/shard_map/all_to_all | solution.py:26
  503.0 7.2 %all-to-all-start.6 = ((f32[16,1,512]{2,1,0:T(1,128)}), f32[16,1,512]{2,1,0:T(1,128)S(1)}, u32[]{:S(2)}, u32[]{:S(2)}) async-start(f32[16,1,512]{2,1,0:T(1,128)} %broadcast_in_dim.63), calls=%async_computation.7 | async-start | bytes 65536 | tf_op jit(solution)/shard_map/all_to_all | solution.py:26
  510.3 5.4 fusion.6
  515.7 1.9 copy.87
  517.5 5.8 %all-to-all-start.5 = ((bf16[16,128,512]{1,2,0:T(8,128)(2,1)}), bf16[16,128,512]{1,2,0:T(8,128)(2,1)S(1)}, u32[]{:S(2)}, u32[]{:S(2)}) async-start(bf16[16,128,512]{1,2,0:T(8,128)(2,1)} %bitcast.40), calls=%async_computation.6 | async-start | bytes 4194304 | tf_op jit(solution)/shard_map/all_to_all | solution.py:59
  523.9 27.7 %all-to-all-done.5 = bf16[16,128,512]{1,2,0:T(8,128)(2,1)S(1)} async-done(((bf16[16,128,512]{1,2,0:T(8,128)(2,1)}), bf16[16,128,512]{1,2,0:T(8,128)(2,1)S(1)}, u32[]{:S(2)}, u32[]{:S(2)}) %all-to-all-start.5) | async-done | bytes 2097184 | tf_op jit(solution)/shard_map/all_to_all | solution.py:59
  (60 shorter events, 7.2 us)
Async XLA Ops:
  7.2 2.2 copy-start.4
  7.2 123.6 %all-gather.8.cloned.1.call-start = ((), (), s32[]{:S(2)}) async-start(), calls=%async_computation.10 | async-start | bytes 9437184 | tf_op jit(solution)/shard_map/all_gather | solution.py:81
  7.9 3.3 copy-start
  7.9 222.4 %all-gather.6.cloned.1.call-start = ((), (), s32[]{:S(2)}) async-start(), calls=%async_computation.9 | async-start | bytes 17825792 | tf_op jit(solution)/shard_map/all_gather | solution.py:16
  10.5 353.9 %all-gather.4.cloned.1.call-start = ((), (), s32[]{:S(2)}) async-start(), calls=%async_computation.8 | async-start | bytes 2228224 | tf_op jit(solution)/shard_map/all_gather | solution.py:122
  11.3 2.6 copy-start.7
  246.4 26.3 %all-to-all-start.2 = ((f32[8,1,1024]{2,1,0:T(1,128)}), f32[8,1,1024]{2,1,0:T(1,128)S(1)}, u32[]{:S(2)}, u32[]{:S(2)}) async-start(f32[8,1,1024]{2,1,0:T(1,128)} %broadcast_in_dim.34), calls=%async_computation.2 | async-start | bytes 65536 | tf_op jit(solution)/shard_map/all_to_all | solution.py:26
  252.7 203.5 %reduce-scatter.2.cloned.1.call-start = ((), (), s32[]{:S(2)}) async-start(), calls=%async_computation.11 | async-start | bytes 9437184 | tf_op jit(solution)/shard_map/reduce_scatter | solution.py:101
  260.5 12.2 %copy-start.1 = (bf16[1024,1024]{0,1:T(8,128)(2,1)S(1)}, bf16[1024,1024]{0,1:T(8,128)(2,1)}, u32[]{:S(2)}) copy-start(bf16[1024,1024]{0,1:T(8,128)(2,1)} %copy.67) | copy-start | bytes 6291460
  288.1 1.0 copy-start.3
  291.8 6.7 %copy-start.5 = (s32[16384]{0:T(1024)S(1)}, s32[16384]{0:T(1024)}, u32[]{:S(2)}) copy-start(s32[16384]{0:T(1024)} %param.21) | copy-start | bytes 196612
  291.8 6.9 %copy-start.6 = (s32[1024]{0:T(1024)S(1)}, s32[1024]{0:T(1024)}, u32[]{:S(2)}) copy-start(s32[1024]{0:T(1024)} %param.20) | copy-start | bytes 12292
  291.8 72.6 %all-to-all-start = ((bf16[8,1024,256]{1,2,0:T(8,128)(2,1)}), bf16[8,1024,256]{1,2,0:T(8,128)(2,1)}, u32[]{:S(2)}, u32[]{:S(2)}) async-start(bf16[8,1024,256]{1,2,0:T(8,128)(2,1)} %stack.2), calls=%async_computation | async-start | bytes 8388608 | tf_op jit(solution)/shard_map/all_to_all | solution.py:116
  298.8 7.1 %copy-start.2 = (bf16[1024,512]{1,0:T(8,128)(2,1)S(1)}, bf16[1024,512]{1,0:T(8,128)(2,1)}, u32[]{:S(2)}) copy-start(bf16[1024,512]{1,0:T(8,128)(2,1)} %param.16) | copy-start | bytes 3145732
  371.6 91.4 %all-to-all-start.1 = ((f32[8,1,1024]{2,1,0:T(1,128)}), f32[8,1,1024]{2,1,0:T(1,128)S(1)}, u32[]{:S(2)}, u32[]{:S(2)}) async-start(f32[8,1,1024]{2,1,0:T(1,128)} %broadcast_in_dim.32), calls=%async_computation.1 | async-start | bytes 65536 | tf_op jit(solution)/shard_map/all_to_all | solution.py:26
  461.8 7.1 %copy-start.8 = (bf16[512]{0:T(512)(128)(2,1)S(1)}, bf16[512]{0:T(512)(128)(2,1)}, u32[]{:S(2)}) copy-start(bf16[512]{0:T(512)(128)(2,1)} %param.19) | copy-start | bytes 3076
  463.0 22.8 %all-to-all-start.3 = ((bf16[16,64,513]{2,1,0:T(8,128)(2,1)}), bf16[16,64,513]{2,1,0:T(8,128)(2,1)S(1)}, u32[]{:S(2)}, u32[]{:S(2)}) async-start(bf16[16,64,513]{2,1,0:T(8,128)(2,1)} %pad_maximum_fusion), calls=%async_computation.4 | async-start | bytes 2621440 | tf_op jit(solution)/shard_map/all_to_all | solution.py:40
  503.0 14.5 %all-to-all-start.6 = ((f32[16,1,512]{2,1,0:T(1,128)}), f32[16,1,512]{2,1,0:T(1,128)S(1)}, u32[]{:S(2)}, u32[]{:S(2)}) async-start(f32[16,1,512]{2,1,0:T(1,128)} %broadcast_in_dim.63), calls=%async_computation.7 | async-start | bytes 65536 | tf_op jit(solution)/shard_map/all_to_all | solution.py:26
  517.5 34.1 %all-to-all-start.5 = ((bf16[16,128,512]{1,2,0:T(8,128)(2,1)}), bf16[16,128,512]{1,2,0:T(8,128)(2,1)S(1)}, u32[]{:S(2)}, u32[]{:S(2)}) async-start(bf16[16,128,512]{1,2,0:T(8,128)(2,1)} %bitcast.40), calls=%async_computation.6 | async-start | bytes 4194304 | tf_op jit(solution)/shard_map/all_to_all | solution.py:59
Sparse Core Ops, SparseCore 0:
  10.2 120.5 all-gather.7
  132.4 97.8 all-gather.5
  232.0 33.8 all-gather.3
  288.3 167.8 reduce-scatter.1
